TPU v7x, 256 devices: a whole 4x4x8 slice. The times are simulated.
256 devices in a mesh: seq: 16 (over z, x_lo), img: 8 (over y, x_hi), fsdp: 2 (over core).
Axes of the slice: x: 4 (x_hi: 2, x_lo: 2; x = x_hi * 2 + x_lo), y: 4, z: 8, core: 2. Of those that a mesh axis runs over, the one named last changes fastest.
Arguments:
- vision_feats: bfloat16 [8, 2304, 1024], P('img', ('seq', 'fsdp')), may hold values from -6 to 6
- ln_gain: float32 [1024], replicated, may hold values from 0.5 to 1.5
- ln_bias: float32 [1024], replicated, may hold values from -3 to 3
- w_in: bfloat16 [1024, 4096], P('fsdp', 'seq'), may hold values from -0.1875 to 0.1875
- b_in: float32 [4096], P('seq'), may hold values from -3 to 3
- w_out: bfloat16 [4096, 4096], P('seq', 'fsdp'), may hold values from -0.09375 to 0.09375
- lm_grad: bfloat16 [8, 4096, 4096], P('img', 'seq', 'fsdp'), may hold values from -0.079589844 to 0.079589844
- image_counts: int32 [8, 2], P('img'), may hold values from 1 to 3, as said below
- token_pos: int32 [8, 2304], P('img'), may hold values from 0 to 2047, as said below
Outputs:
- w_in_grad: float32 [1024, 4096], P(('img', 'fsdp'), 'seq')
- b_in_grad: float32 [4096], replicated
- w_out_grad: float32 [4096, 4096], P(('seq', 'img'), 'fsdp')
- b_out_grad: float32 [4096], replicated
- ln_gain_grad: float32 [1024], replicated
- ln_bias_grad: float32 [1024], replicated
Inputs may be any that keep to these rules, and one draw needn't show every extreme that they name: `image_counts`: in each group the 2 samples hold 4 images together, each sample one or more. `token_pos`: each image's 576 tokens take consecutive positions of its sample's sequence in order; a sample's images come in order without intersection, and images are numbered sample by sample as image_counts gives.
All inputs are finite; a program needn't handle non-finite values.
Results may differ from a plain program's by a relative error of at most 0.0047.
Values may be sent and summed in bfloat16 or wider, within the bound.
No kernel may reach another device: no remote copies, remote signals or barrier semaphores. Data moves between devices by JAX's collectives and lax.ppermute only.
A program may use at most 128 MiB of HBM per device.

v0:
```python
import jax
import jax.numpy as jnp
from jax import lax
from jax.sharding import Mesh
from jax.sharding import PartitionSpec as P

PATCH = 576
LEN = 2048
SEQ = ("seq_0", "seq_1")
IMG = ("img_0", "img_1")
SEQ_FSDP = ("seq_0", "seq_1", "fsdp")
SEQ_IMG_FSDP = ("seq_0", "seq_1", "img_0", "img_1", "fsdp")
IMG_FSDP = ("img_0", "img_1", "fsdp")
SEQ_IMG = ("seq_0", "seq_1", "img_0", "img_1")


def copy_for_each(array, axis):
    copies = jnp.broadcast_to(array, (lax.axis_size(axis), *array.shape))
    return lax.all_to_all(copies, axis, split_axis=0, concat_axis=0, tiled=True)


def in_order(pieces, dim):
    shape = list(pieces.shape[1:])
    shape[dim] *= pieces.shape[0]
    return jnp.moveaxis(pieces, 0, dim).reshape(shape)


def gather_directly(array, axis, dim):
    pieces = copy_for_each(array, axis)
    return in_order(pieces, dim)


def whole_of(array, axes, dim):
    if not axes:
        return array
    nearer = lax.all_gather(array, axes[-1], axis=dim, tiled=True)
    return whole_of(nearer, axes[:-1], dim)


def taken_together(array, axis):
    return copy_for_each(array, axis).sum(axis=0)


def in_blocks(array, dim, devices):
    shape = array.shape
    pieces = array.reshape(*shape[:dim], devices, shape[dim] // devices, *shape[dim + 1 :])
    return jnp.moveaxis(pieces, dim, 0)


def one_scatter(arrays, axis, dims):
    devices = lax.axis_size(axis)
    pieces = [in_blocks(a, dim, devices) for a, dim in zip(arrays, dims)]
    lines = jnp.concatenate([b.reshape(devices, -1) for b in pieces], axis=1)
    width = max(16, -(-lines.shape[1] // 1024) * 8)
    lines = jnp.pad(lines, ((0, 0), (0, width * 128 - lines.shape[1]))).reshape(-1, 128)
    vector, at, gathered = (lax.psum_scatter(lines, axis, tiled=True).reshape(-1), 0, [])
    for b in pieces:
        part = b[0]
        gathered.append(vector[at : at + part.size].reshape(part.shape))
        at += part.size
    return tuple(gathered)


def one_axis_at_a_time(array, axes):
    for axis in axes:
        array = lax.psum(array, axis)
    return array


def gelu_parts(preact):
    cumul = 0.5 * (1.0 + lax.erf(preact * 0.7071067811865476))
    density = jnp.exp(-0.5 * preact * preact) * 0.3989422804014327
    return (preact * cumul, cumul + preact * density)


def contract(left, right, left_dim, right_dim):
    return lax.dot_general(
        left, right, (((left_dim,), (right_dim,)), ((), ())), preferred_element_type=jnp.float32
    )


def own_columns(matrix, img_count, fsdp_count, fsdp_index):
    rows = matrix.shape[0]
    block = matrix.shape[1] // (img_count * fsdp_count)
    shaped = matrix.reshape(rows, img_count, fsdp_count, block)
    taken = lax.dynamic_index_in_dim(shaped, fsdp_index, axis=2, keepdims=False)
    return taken.reshape(rows, img_count * block)


def place_columns(vector, img_count, fsdp_count, fsdp_index):
    block = vector.shape[0] // img_count
    holder = jnp.zeros((img_count, fsdp_count, block), jnp.float32)
    holder = lax.dynamic_update_slice(
        holder, vector.reshape(img_count, 1, block), (0, fsdp_index, 0)
    )
    return holder.reshape(img_count * fsdp_count * block)


def per_device(vision_feats, ln_gain, ln_bias, w_in, b_in, w_out, lm_grad, image_counts, token_pos):
    seq_count = lax.axis_size(SEQ)
    seq_index = lax.axis_index(SEQ)
    img_count = lax.axis_size(IMG)
    fsdp_count = lax.axis_size("fsdp")
    fsdp_index = lax.axis_index("fsdp")
    lm_block = lm_grad[0]
    block_rows = lm_block.shape[0]
    half_width = lm_block.shape[1]
    position_count = block_rows * seq_count
    counts = image_counts[0]
    positions = token_pos[0]
    row_count = positions.shape[0]
    image_index = jnp.arange(row_count, dtype=jnp.int32) // PATCH
    bounds = jnp.cumsum(counts)
    sample = jnp.sum((image_index[:, None] >= bounds[None, :]).astype(jnp.int32), axis=1)
    abs_pos = sample * LEN + positions
    marker = jnp.zeros((position_count,), jnp.float32).at[abs_pos].set(1.0)
    own_mask = lax.dynamic_slice_in_dim(marker, seq_index * block_rows, block_rows).astype(
        jnp.bfloat16
    )
    out_bias_half = jnp.dot(own_mask[None, :], lm_block, preferred_element_type=jnp.float32)[0]
    out_bias_full = lax.dynamic_update_slice_in_dim(
        jnp.zeros((half_width * fsdp_count,), jnp.float32),
        out_bias_half,
        fsdp_index * half_width,
        0,
    )
    w_in_full = gather_directly(w_in, "fsdp", 0)
    gathered = lax.all_gather(vision_feats[0], SEQ_FSDP, axis=0, tiled=True)
    values = gathered.astype(jnp.float32)
    row_mean = jnp.mean(values, axis=1, keepdims=True)
    centred = values - row_mean
    row_var = jnp.mean(centred * centred, axis=1, keepdims=True)
    normed = centred * lax.rsqrt(row_var + 1e-05)
    normed_in = (normed * ln_gain + ln_bias).astype(jnp.bfloat16)
    preact = jnp.dot(normed_in, w_in_full, preferred_element_type=jnp.float32) + b_in
    activ, slope = gelu_parts(preact)
    hidden = activ.astype(jnp.bfloat16)
    hidden_width = hidden.shape[1]
    whole_grad = whole_of(lm_block, SEQ, 0)
    picked = whole_grad[abs_pos]
    hidden_part = contract(picked, w_out, 1, 1)
    w_out_part = contract(hidden, picked, 0, 0)
    hidden_grad = taken_together(hidden_part, "fsdp")
    preact_grad = (hidden_grad * slope).astype(jnp.bfloat16)
    own_normed_in = own_columns(normed_in, img_count, fsdp_count, fsdp_index)
    own_normed = own_columns(normed, img_count, fsdp_count, fsdp_index)
    own_w_in = own_columns(w_in_full.T, img_count, fsdp_count, fsdp_index)
    w_in_part = contract(own_normed_in, preact_grad, 0, 0)
    half_rows = row_count // fsdp_count
    own_rows = lax.dynamic_slice_in_dim(preact_grad, fsdp_index * half_rows, half_rows, 0)
    b_in_part = jnp.sum(own_rows, axis=0, dtype=jnp.float32)
    normed_grad = contract(preact_grad, own_w_in, 1, 0)
    gain_part = place_columns(
        jnp.sum(normed_grad * own_normed, axis=0), img_count, fsdp_count, fsdp_index
    )
    bias_part = place_columns(jnp.sum(normed_grad, axis=0), img_count, fsdp_count, fsdp_index)
    w_in_grad, w_out_grad = one_scatter((w_in_part, w_out_part), IMG, (0, 0))
    hidden_full = lax.dynamic_update_slice_in_dim(
        jnp.zeros((hidden_width * seq_count,), jnp.float32), b_in_part, seq_index * hidden_width, 0
    )
    gain_grad, bias_grad, b_in_grad, b_out_grad = (
        one_axis_at_a_time(gain_part, SEQ_IMG_FSDP),
        one_axis_at_a_time(bias_part, SEQ_IMG_FSDP),
        one_axis_at_a_time(hidden_full, SEQ_IMG_FSDP),
        one_axis_at_a_time(out_bias_full, SEQ_IMG_FSDP),
    )
    return (w_in_grad, b_in_grad, w_out_grad, b_out_grad, gain_grad, bias_grad)


def solution(mesh):
    finer = Mesh(
        mesh.devices.reshape(8, 2, 4, 2, mesh.shape["fsdp"]),
        ("seq_0", "seq_1", "img_0", "img_1", "fsdp"),
    )
    placed = (
        P(IMG, SEQ_FSDP, None),
        P(),
        P(),
        P("fsdp", SEQ),
        P(SEQ),
        P(SEQ, "fsdp"),
        P(IMG, SEQ, "fsdp"),
        P(IMG, None),
        P(IMG, None),
    )
    return jax.shard_map(
        per_device,
        mesh=finer,
        in_specs=placed,
        out_specs=(P(IMG_FSDP, SEQ), P(), P(SEQ_IMG, "fsdp"), P(), P(), P()),
        check_vma=False,
    )
```

profile of v0, /device:TPU:1, one launch (start us, length us, event | category | flops | bytes accessed | tf_op | source)
XLA Modules:
  0.0 471.8 jit_solution(9273449355537463096)
XLA Ops:
  7.2 0.0 copy-start
  7.2 0.0 copy-start.13
  7.2 0.0 copy-start.9
  7.2 0.0 all-gather.9.cloned.1.call-start
  7.3 0.7 all-gather.9.cloned.1.call-update
  7.9 0.0 all-gather.7.cloned.1.call-start
  8.0 0.7 all-gather.7.cloned.1.call-update
  8.7 0.0 all-gather.11.cloned.1.call-start
  8.7 42.9 %all-gather.9.cloned.1.call-done = bf16[1,512,2048]{2,1,0:T(8,128)(2,1)} async-done(((bf16[1,256,2048]{2,1,0:T(8,128)(2,1)}), bf16[1,512,2048]{2,1,0:T(8,128)(2,1)}) %all-gather.9.cloned.1.call-update) | async-done | bytes 2097168 | tf_op jit(solution)/shard_map/all_gather | solution.py:36
  51.6 0.0 all-gather.11.cloned.1.call-update
  51.7 0.2 reduce-window.8
  51.9 0.1 fusion.13
  52.0 70.0 %all-gather.7.cloned.1.call-done = bf16[1,2304,1024]{2,1,0:T(8,128)(2,1)} async-done(((bf16[1,72,1024]{2,1,0:T(8,128)(2,1)}), bf16[1,2304,1024]{2,1,0:T(8,128)(2,1)}) %all-gather.7.cloned.1.call-update) | async-done | bytes 4718608 | tf_op jit(solution)/shard_map/all_gather | solution.py:128
  122.1 6.8 %copy.20 = bf16[1,2304,1024]{1,2,0:T(8,128)(2,1)} copy(bf16[1,2304,1024]{2,1,0:T(8,128)(2,1)} %all-gather.7.cloned.1.call-done) | data formatting | bytes 9437184 | tf_op jit(solution)/shard_map/all_gather | solution.py:128
  128.9 3.2 convert_reduce_fusion
  132.1 0.6 copy-done.2
  132.6 1.3 fusion.3
  133.9 4.8 %fusion.1 = (f32[2304,1024]{0,1:T(8,128)}, bf16[2304,1024]{0,1:T(8,128)(2,1)S(1)}) fusion(bf16[1,2304,1024]{1,2,0:T(8,128)(2,1)S(1)} %copy-done.2, f32[2304]{0:T(1024)S(1)} %add_rsqrt_fusion, f32[2304]{0:T(1024)S(1)} %broadcast_multiply_fusion.1, f32[1024]{0:T(1024)S(1)} %copy-done.10, f32[1024]{0:T(1024)S(1)} %copy-done.11), kind=kLoop, calls=%fused_computation.5 | loop fusion | flops 14155776 | bytes 18900992 | tf_op jit(solution)/shard_map/mul | solution.py:133
  138.7 2.1 copy-done.3
  140.9 1.6 constant_dynamic-slice_fusion.2
  142.5 153.5 %all-gather.11.cloned.1.call-done = bf16[1,4096,2048]{2,1,0:T(8,128)(2,1)} async-done(((bf16[1,512,2048]{2,1,0:T(8,128)(2,1)}), bf16[1,4096,2048]{2,1,0:T(8,128)(2,1)}) %all-gather.11.cloned.1.call-update) | async-done | bytes 16777232 | tf_op jit(solution)/shard_map/all_gather | solution.py:36
  296.0 26.2 %gather_fusion = bf16[2304,2048]{1,0:T(8,128)(2,1)} fusion(bf16[4096,2048]{1,0:T(8,128)(2,1)} %bitcast.43, s32[3072]{0:T(1024)S(1)} %pad_clamp_fusion), kind=kCustom, calls=%fused_computation | custom fusion | bytes 18883584 | tf_op jit(solution)/shard_map/gather | solution.py:140
  322.2 5.2 %fusion.21 = f32[2304,256]{1,0:T(8,128)S(1)} fusion(bf16[2304,2048]{1,0:T(8,128)(2,1)} %gather_fusion, bf16[256,2048]{1,0:T(8,128)(2,1)S(1)} %copy-done), kind=kOutput, calls=%fused_computation.48 | convolution fusion | flops 2415919104 | bytes 12845056 | tf_op jit(solution)/shard_map/dot_general | solution.py:77
  327.5 0.3 broadcast_in_dim.6
  327.8 0.0 copy-start.8
  327.8 9.2 %all_to_all.10 = f32[2,2304,256]{2,1,0:T(8,128)} all-to-all(f32[2,2304,256]{2,1,0:T(8,128)S(1)} %broadcast_in_dim.6), channel_id=1, replica_groups=mesh['seq_0'=8,'seq_1'=2,'img_0'=4,'img_1'=2,'fsdp'=2] {'fsdp'}, dimensions={0} | all-to-all | bytes 9437184 | tf_op jit(solution)/shard_map/all_to_all | solution.py:19
  337.0 0.0 copy-done.8
  337.0 0.8 broadcast_in_dim.7
  337.9 3.8 all-to-all-start.1
  341.7 0.0 reduce-scatter.2.cloned.1.call-start
  341.7 4.5 reduce_sum.66
  346.2 0.0 all-to-all-done.1
  346.2 0.0 slice-start.2
  346.2 6.7 %fusion.9 = (bf16[2304,256]{1,0:T(8,128)(2,1)}, f32[2304,256]{1,0:T(8,128)S(1)}) fusion(f32[2304,256]{1,0:T(8,128)} %reduce_sum.66, f32[256]{0:T(256)S(1)} %copy-done.12, bf16[2304,1024]{0,1:T(8,128)(2,1)} %copy-done.3, bf16[1024,256]{1,0:T(8,128)(2,1)S(1)} %bitcast.50), kind=kOutput, calls=%fused_computation.18 | convolution fusion | flops 1214447616 | bytes 11142144 | tf_op jit(solution)/shard_map/dot_general | solution.py:135
  352.9 4.0 fusion.10
  356.9 2.0 reshape_reshape.7
  358.9 2.8 fusion.22
  361.7 0.1 reshape_reshape.6
  361.8 1.7 pad_maximum_fusion
  363.5 3.6 reshape.151
  367.1 0.0 reduce-scatter.2.cloned.1.call-update
  367.1 9.0 %scatter_custom_fusion = f32[4096]{0:T(1024)S(1)} fusion(s32[2304]{0:T(1024)S(1)} %fusion.17, f32[2304]{0:T(1024)S(1)} %broadcast.81, f32[]{:T(128)} %constant.22.clone.1), kind=kCustom, calls=%fused_computation.39 | custom fusion | bytes 16388 | tf_op jit(solution)/shard_map/scatter | solution.py:116
  376.1 0.1 dynamic_slice.28
  376.2 0.0 copy-done.4
  376.2 0.2 fusion.11
  376.5 0.2 dynamic_update_slice.13
  376.7 5.0 %constant_dynamic-slice_fusion = f32[2304,8,1,64]{0,3,2,1:T(8,128)} fusion(f32[2304,8,2,64]{0,3,2,1:T(8,128)} %bitcast.46, s32[]{:T(128)S(6)} %select_n.40), kind=kLoop, calls=%fused_computation.44 | loop fusion | bytes 9437188 | tf_op jit(solution)/shard_map/jit(dynamic_index_in_dim)/dynamic_slice | solution.py:86
  381.8 6.2 %copy.21 = f32[2304,512]{1,0:T(8,128)} copy(f32[2304,512]{0,1:T(8,128)} %bitcast.47) | data formatting | bytes 9437184 | tf_op jit(solution)/shard_map/reshape | solution.py:87
  388.0 3.3 fusion.20
  391.3 0.1 reshape.158
  391.5 0.1 reshape.159
  391.5 0.1 reshape.160
  391.7 0.1 reshape.161
  391.7 0.2 convert_reduce_fusion.1
  391.9 0.3 dynamic_update_slice.12
  392.2 23.3 %all-reduce = (f32[4096]{0:T(1024)S(1)}, f32[4096]{0:T(1024)S(1)}, f32[1024]{0:T(1024)S(1)}, f32[1024]{0:T(1024)S(1)}) all-reduce(f32[4096]{0:T(1024)S(1)} %dynamic_update_slice.12, f32[4096]{0:T(1024)S(1)} %dynamic_update_slice.13, ...), channel_id=1, replica_groups=mesh['seq_0'=8,'seq_1'=2,'img_0'=4,'img_1'=2,'fsdp'=2] {'seq_0'}, use_global_device_ids=true, to_apply=%region_7.8 | all-reduce | flops 10240 | bytes 81920 | tf_op jit(solution)/shard_map/psum | solution.py:66
  415.5 5.9 %all-reduce.4 = (f32[4096]{0:T(1024)S(1)}, f32[4096]{0:T(1024)S(1)}, f32[1024]{0:T(1024)S(1)}, f32[1024]{0:T(1024)S(1)}) all-reduce(f32[4096]{0:T(1024)S(1)} %get-tuple-element.8, f32[4096]{0:T(1024)S(1)} %get-tuple-element.9, ...), channel_id=1, replica_groups=mesh['seq_0'=8,'seq_1'=2,'img_0'=4,'img_1'=2,'fsdp'=2] {'seq_1'}, use_global_device_ids=true, to_apply=%region_8.9 | all-reduce | flops 10240 | bytes 81920 | tf_op jit(solution)/shard_map/psum | solution.py:66
  421.4 14.4 %all-reduce.1 = (f32[4096]{0:T(1024)S(1)}, f32[4096]{0:T(1024)S(1)}, f32[1024]{0:T(1024)S(1)}, f32[1024]{0:T(1024)S(1)}) all-reduce(f32[4096]{0:T(1024)S(1)} %get-tuple-element.24, f32[4096]{0:T(1024)S(1)} %get-tuple-element.25, ...), channel_id=1, replica_groups=mesh['seq_0'=8,'seq_1'=2,'img_0'=4,'img_1'=2,'fsdp'=2] {'img_0'}, use_global_device_ids=true, to_apply=%region_9.10 | all-reduce | flops 10240 | bytes 81920 | tf_op jit(solution)/shard_map/psum | solution.py:66
  435.7 10.3 %all-reduce.3 = (f32[4096]{0:T(1024)S(1)}, f32[4096]{0:T(1024)S(1)}, f32[1024]{0:T(1024)S(1)}, f32[1024]{0:T(1024)S(1)}) all-reduce(f32[4096]{0:T(1024)S(1)} %get-tuple-element.12, f32[4096]{0:T(1024)S(1)} %get-tuple-element.13, ...), channel_id=1, replica_groups=mesh['seq_0'=8,'seq_1'=2,'img_0'=4,'img_1'=2,'fsdp'=2] {'img_1'}, use_global_device_ids=true, to_apply=%region_10.11 | all-reduce | flops 10240 | bytes 81920 | tf_op jit(solution)/shard_map/psum | solution.py:66
  446.0 16.1 %all-reduce.2 = (f32[4096]{0:T(1024)}, f32[4096]{0:T(1024)}, f32[1024]{0:T(1024)}, f32[1024]{0:T(1024)}) all-reduce(f32[4096]{0:T(1024)S(1)} %get-tuple-element.20, f32[4096]{0:T(1024)S(1)} %get-tuple-element.21, f32[1024]{0:T(1024)S(1)} %get-tuple-element.22, ...), channel_id=1, replica_groups=mesh['seq_0'=8,'seq_1'=2,'img_0'=4,'img_1'=2,'fsdp'=2] {'fsdp'}, use_global_device_ids=true, to_apply=%region_11.12 | all-reduce | flops 10240 | bytes 81920 | tf_op jit(solution)/shard_map/psum | solution.py:66
  462.1 0.8 slice.12
  462.9 0.6 reshape.152
  463.6 1.0 slice.13
  464.6 0.7 reshape.153
  (42 shorter events, 0.2 us)
Async XLA Ops:
  7.2 315.1 %copy-start = (bf16[256,2048]{1,0:T(8,128)(2,1)S(1)}, bf16[256,2048]{1,0:T(8,128)(2,1)}, u32[]{:S(2)}) copy-start(bf16[256,2048]{1,0:T(8,128)(2,1)} %param.14) | copy-start | bytes 3145732
  7.2 44.5 %copy-start.13 = (s32[1,2]{1,0:T(1,128)S(1)}, s32[1,2]{1,0:T(1,128)}, u32[]{:S(2)}) copy-start(s32[1,2]{1,0:T(1,128)} %param.16) | copy-start | bytes 28
  7.2 44.8 %copy-start.9 = (s32[1,2304]{1,0:T(1,128)S(1)}, s32[1,2304]{1,0:T(1,128)}, u32[]{:S(2)}) copy-start(s32[1,2304]{1,0:T(1,128)} %param.17) | copy-start | bytes 27652
  7.2 44.4 %all-gather.9.cloned.1.call-start = ((), (), s32[]{:S(2)}) async-start(), calls=%async_computation.5 | async-start | bytes 3145728 | tf_op jit(solution)/shard_map/all_gather | solution.py:36
  7.9 114.2 %all-gather.7.cloned.1.call-start = ((), (), s32[]{:S(2)}) async-start(), calls=%async_computation.4 | async-start | bytes 4866048 | tf_op jit(solution)/shard_map/all_gather | solution.py:128
  8.7 287.3 %all-gather.11.cloned.1.call-start = ((), (), s32[]{:S(2)}) async-start(), calls=%async_computation.6 | async-start | bytes 18874368 | tf_op jit(solution)/shard_map/all_gather | solution.py:36
  128.9 3.8 copy-start.2
  132.6 1.3 copy-start.10
  132.6 1.3 copy-start.11
  138.7 2.1 copy-start.3
  327.8 9.2 %copy-start.8 = (bf16[512,256]{1,0:T(8,128)(2,1)S(1)}, bf16[512,256]{1,0:T(8,128)(2,1)}, u32[]{:S(2)}) copy-start(bf16[512,256]{1,0:T(8,128)(2,1)} %param.12) | copy-start | bytes 786436
  337.9 8.3 %all-to-all-start.1 = ((bf16[2,512,256]{2,1,0:T(8,128)(2,1)}), bf16[2,512,256]{2,1,0:T(8,128)(2,1)S(1)}, u32[]{:S(2)}, u32[]{:S(2)}) async-start(bf16[2,512,256]{2,1,0:T(8,128)(2,1)} %broadcast_in_dim.7), calls=%async_computation.1 | async-start | bytes 1048576 | tf_op jit(solution)/shard_map/all_to_all | solution.py:19
  341.7 4.5 copy-start.12
  341.7 120.4 %reduce-scatter.2.cloned.1.call-start = ((), (), s32[]{:S(2)}) async-start(), calls=%async_computation.3 | async-start | bytes 2949120 | tf_op jit(solution)/shard_map/reduce_scatter | solution.py:56
  341.7 11.2 %slice-start = ((s8[9437184]{0:T(1024)(128)(4,1)}), s8[1048576]{0:T(1024)(128)(4,1)S(1)}, s32[]{:S(2)}) async-start(s8[9437184]{0:T(1024)(128)(4,1)} %bitcast.44), calls=%async_computation.7 | async-start | bytes 2097152
  346.2 6.7 %copy-start.6 = (bf16[2,512,256]{2,1,0:T(8,128)(2,1)}, bf16[2,512,256]{2,1,0:T(8,128)(2,1)S(1)}, u32[]{:S(2)}) copy-start(bf16[2,512,256]{2,1,0:T(8,128)(2,1)S(1)} %all-to-all-done.1) | copy-start | bytes 1572868
  346.2 6.7 %slice-start.1 = ((s8[9437184]{0:T(1024)(128)(4,1)}), s8[4194304]{0:T(1024)(128)(4,1)S(1)}, s32[]{:S(2)}) async-start(s8[9437184]{0:T(1024)(128)(4,1)} %bitcast.44), calls=%async_computation.8 | async-start | bytes 8388608
  346.2 6.7 %slice-start.2 = ((s8[9437184]{0:T(1024)(128)(4,1)}), s8[4194304]{0:T(1024)(128)(4,1)S(1)}, s32[]{:S(2)}) async-start(s8[9437184]{0:T(1024)(128)(4,1)} %bitcast.44), calls=%async_computation.9 | async-start | bytes 8388608
  367.1 9.1 %copy-start.4 = (bf16[1,256,2048]{2,1,0:T(8,128)(2,1)S(1)}, bf16[1,256,2048]{2,1,0:T(8,128)(2,1)}, u32[]{:S(2)}) copy-start(bf16[1,256,2048]{2,1,0:T(8,128)(2,1)} %param.15) | copy-start | bytes 3145732
  367.1 9.6 %copy-start.7 = (bf16[2,512,256]{2,1,0:T(8,128)(2,1)S(1)}, bf16[2,512,256]{2,1,0:T(8,128)(2,1)}, u32[]{:S(2)}) copy-start(bf16[2,512,256]{2,1,0:T(8,128)(2,1)} %copy-done.6) | copy-start | bytes 1572868
  381.8 6.3 %copy-start.5 = (bf16[2304,256]{1,0:T(8,128)(2,1)S(1)}, bf16[2304,256]{1,0:T(8,128)(2,1)}, u32[]{:S(2)}) copy-start(bf16[2304,256]{1,0:T(8,128)(2,1)} %get-tuple-element.30) | copy-start | bytes 3538948
  388.0 77.3 %copy-start.1 = (bf16[256,2048]{1,0:T(8,128)(2,1)S(1)}, bf16[256,2048]{1,0:T(8,128)(2,1)}, u32[]{:S(2)}) copy-start(bf16[256,2048]{1,0:T(8,128)(2,1)} %param.14) | copy-start | bytes 3145732
Sparse Core Ops, SparseCore 0:
  9.8 41.7 all-gather.8
  53.5 68.5 all-gather.6
  123.9 172.0 all-gather.10
  367.2 79.7 reduce-scatter.1
where the time goes:
time: 473 us; the launch traced here: 472 us
  waiting for transfers between devices  268 us (57%)
  blocking collectives  79.1 us (17%)
  local copies, waits for them, and re-layouts  68.7 us (15%)
  matrix products  22.2 us (5%)
  other arithmetic  16 us (3%)
  between operations  14 us (3%)
    all_gather x2, waiting for transfers between devices, whole_of(): nearer = lax.all_gather(array, axes[-1], axis=dim, tiled=True)  196 us
    all_gather x1, waiting for transfers between devices, per_device(): gathered = lax.all_gather(vision_feats[0], SEQ_FSDP, axis=0, tiled=True)  70 us
    psum x5, blocking collectives, one_axis_at_a_time(): array = lax.psum(array, axis)  69.9 us
    gather x1, local copies, waits for them, and re-layouts, per_device(): picked = whole_grad[abs_pos]  26.2 us
    dot_general x4, matrix products, contract(): lax.dot_general(left, right, (((left_dim,), (right_dim,)), ((), ())), pre...  15.2 us
  transfers between devices with their start and end apart: 5, of which 3 were waited for; matrix products, arithmetic and copies ran while one was open for 10% of the time, Pallas kernels for 0%

commit v1 on v0

--- a/solution.py
+++ b/solution.py
@@ -125,7 +125,11 @@
         0,
     )
     w_in_full = gather_directly(w_in, "fsdp", 0)
-    gathered = lax.all_gather(vision_feats[0], SEQ_FSDP, axis=0, tiled=True)
+    x = vision_feats[0]
+    count = lax.axis_size(SEQ_FSDP)
+    shards = jnp.stack([x for _ in range(count)])
+    shards = lax.all_to_all(shards, SEQ_FSDP, split_axis=0, concat_axis=0)
+    gathered = jnp.concatenate(shards, axis=0)
     values = gathered.astype(jnp.float32)
     row_mean = jnp.mean(values, axis=1, keepdims=True)
     centred = values - row_mean

time: 473 us -> 502 us (1.061)
  local copies, waits for them, and re-layouts: 68.7 us -> 101 us
  waiting for transfers between devices: 268 us -> 239 us
  other arithmetic: 16 us -> 32.6 us
  starting transfers between devices: 3.97 us -> 12.1 us
    all_to_all x0 -> x1, waiting for transfers between devices: none -> 157 us  [per_device(): shards = lax.all_to_all(shards, SEQ_FSDP, split_axis=0, concat_axis=0)]
    all_gather x2, waiting for transfers between devices: 196 us -> 81.1 us  [whole_of(): nearer = lax.all_gather(array, axes[-1], axis=dim, tiled=True)]
    all_gather x1 -> x0, waiting for transfers between devices: 70 us -> none  [per_device(): gathered = lax.all_gather(vision_feats[0], SEQ_FSDP, axis=0, tiled=True)]
    convert_element_type x0 -> x2, local copies, waits for them, and re-layouts: none -> 42.9 us  [per_device(): values = gathered.astype(jnp.float32)]
    convert_element_type x0 -> x2, other arithmetic: none -> 13.1 us  [per_device(): normed_in = (normed * ln_gain + ln_bias).astype(jnp.bfloat16)]
    all_to_all x0 -> x1, starting transfers between devices: none -> 8.2 us  [per_device(): shards = lax.all_to_all(shards, SEQ_FSDP, split_axis=0, concat_axis=0)]
    all_gather x1 -> x0, local copies, waits for them, and re-layouts: 6.78 us -> none  [per_device(): gathered = lax.all_gather(vision_feats[0], SEQ_FSDP, axis=0, tiled=True)]
    dynamic_slice x3 -> x2, local copies, waits for them, and re-layouts: 6.68 us -> 0.03 us  [own_columns(): taken = lax.dynamic_index_in_dim(shaped, fsdp_index, axis=2, keepdims=False)]
  transfers between devices with their start and end apart: 5 -> 5, of which waited for: 3 -> 3; matrix products, arithmetic and copies ran while one was open for 10% -> 19% of each run, Pallas kernels for 0% -> 0%
where the time goes in v1:
time: 502 us; the launch traced here: 500 us
  waiting for transfers between devices  239 us (48%)
  local copies, waits for them, and re-layouts  101 us (20%)
  blocking collectives  78.8 us (16%)
  other arithmetic  32.6 us (6%)
  matrix products  23.2 us (5%)
  between operations  14 us (3%)
  starting transfers between devices  12.1 us (2%)
    all_to_all x1, waiting for transfers between devices, per_device(): shards = lax.all_to_all(shards, SEQ_FSDP, split_axis=0, concat_axis=0)  157 us
    all_gather x2, waiting for transfers between devices, whole_of(): nearer = lax.all_gather(array, axes[-1], axis=dim, tiled=True)  81.1 us
    psum x5, blocking collectives, one_axis_at_a_time(): array = lax.psum(array, axis)  69.9 us
    convert_element_type x2, local copies, waits for them, and re-layouts, per_device(): values = gathered.astype(jnp.float32)  42.9 us
    gather x1, local copies, waits for them, and re-layouts, per_device(): picked = whole_grad[abs_pos]  26.3 us
    dot_general x4, matrix products, contract(): lax.dot_general(left, right, (((left_dim,), (right_dim,)), ((), ())), pre...  16.2 us
    convert_element_type x2, other arithmetic, per_device(): normed_in = (normed * ln_gain + ln_bias).astype(jnp.bfloat16)  13.1 us
  transfers between devices with their start and end apart: 5, of which 3 were waited for; matrix products, arithmetic and copies ran while one was open for 19% of the time, Pallas kernels for 0%

profile of v1, /device:TPU:1, one launch (start us, length us, event | category | flops | bytes accessed | tf_op | source)
XLA Modules:
  0.0 500.0 jit_solution(17388294014397632567)
XLA Ops:
  7.2 0.0 copy-start
  7.2 0.0 all-gather.5.cloned.1.call-start
  7.2 0.7 all-gather.5.cloned.1.call-update
  7.9 0.0 all-gather.7.cloned.1.call-start
  8.0 43.6 %all-gather.5.cloned.1.call-done = bf16[1,512,2048]{2,1,0:T(8,128)(2,1)} async-done(((bf16[1,256,2048]{2,1,0:T(8,128)(2,1)}), bf16[1,512,2048]{2,1,0:T(8,128)(2,1)}) %all-gather.5.cloned.1.call-update) | async-done | bytes 2097168 | tf_op jit(solution)/shard_map/all_gather | solution.py:36
  51.6 0.0 all-gather.7.cloned.1.call-update
  51.7 2.7 stack.3
  54.4 8.2 %all-to-all-start = ((bf16[32,72,1024]{2,1,0:T(8,128)(2,1)}), bf16[32,72,1024]{2,1,0:T(8,128)(2,1)}, u32[]{:S(2)}, u32[]{:S(2)}) async-start(bf16[32,72,1024]{2,1,0:T(8,128)(2,1)} %stack.3), calls=%async_computation | async-start | bytes 9437184 | tf_op jit(solution)/shard_map/all_to_all | solution.py:131
  62.6 0.2 reduce-window.8
  62.8 0.1 mul.106
  62.9 0.0 copy-done.8
  62.9 0.1 add.139
  63.0 0.1 fusion.9
  63.1 0.0 copy-done.10
  63.2 156.9 %all-to-all-done = bf16[32,72,1024]{2,1,0:T(8,128)(2,1)} async-done(((bf16[32,72,1024]{2,1,0:T(8,128)(2,1)}), bf16[32,72,1024]{2,1,0:T(8,128)(2,1)}, u32[]{:S(2)}, u32[]{:S(2)}) %all-to-all-start) | async-done | bytes 4718624 | tf_op jit(solution)/shard_map/all_to_all | solution.py:131
  220.0 3.1 convert_reduce_fusion
  223.2 0.1 div.19
  223.3 3.8 multiply_reduce_fusion
  227.1 0.1 rsqrt.13
  227.2 18.0 %reshape.252 = f32[2304,8,2,64]{3,2,1,0:T(2,128)} reshape(bf16[32,72,1024]{2,1,0:T(8,128)(2,1)} %all-to-all-done) | data formatting | bytes 14155776 | tf_op jit(solution)/shard_map/convert_element_type | solution.py:133
  245.2 24.9 %copy.21 = f32[2304,8,2,64]{0,3,2,1:T(8,128)} copy(f32[2304,8,2,64]{3,2,1,0:T(2,128)} %reshape.252) | data formatting | bytes 18874368 | tf_op jit(solution)/shard_map/convert_element_type | solution.py:133
  270.1 6.9 %add_convert_fusion = bf16[32,72,1024]{2,1,0:T(8,128)(2,1)} fusion(bf16[32,72,1024]{2,1,0:T(8,128)(2,1)} %all-to-all-done, f32[1024]{0:T(1024)S(1)} %copy-done.8, f32[1024]{0:T(1024)S(1)} %copy-done.9, f32[32,72]{1,0:T(8,128)S(1)} %add_rsqrt_fusion, f32[32,72]{1,0:T(8,128)S(1)} %broadcast_multiply_fusion), kind=kLoop, calls=%fused_computation.2 | loop fusion | flops 14155776 | bytes 9463808 | tf_op jit(solution)/shard_map/convert_element_type | solution.py:138
  277.0 4.8 subtract_multiply_fusion
  281.8 6.2 %add_convert_fusion.1 = (bf16[2304,8,1,64]{0,3,2,1:T(8,128)(2,1)}, f32[2304,8,1,64]{0,3,2,1:T(8,128)}) fusion(f32[8,1,64]{2,1,0:T(1,128)S(1)} %get-tuple-element.33, f32[8,1,64]{2,1,0:T(1,128)S(1)} %get-tuple-element.32, f32[2304,8,2,64]{0,3,2,1:T(8,128)} %subtract_multiply_fusion, s32[]{:T(128)S(6)} %select_n.40), kind=kLoop, calls=%fused_computation.7 | loop fusion | flops 3538944 | bytes 11800580 | tf_op jit(solution)/shard_map/convert_element_type | solution.py:138
  287.9 37.5 %all-gather.7.cloned.1.call-done = bf16[1,4096,2048]{2,1,0:T(8,128)(2,1)} async-done(((bf16[1,512,2048]{2,1,0:T(8,128)(2,1)}), bf16[1,4096,2048]{2,1,0:T(8,128)(2,1)}) %all-gather.7.cloned.1.call-update) | async-done | bytes 16777232 | tf_op jit(solution)/shard_map/all_gather | solution.py:36
  325.4 26.3 %gather_fusion = bf16[2304,2048]{1,0:T(8,128)(2,1)} fusion(bf16[4096,2048]{1,0:T(8,128)(2,1)} %bitcast.32, s32[3072]{0:T(1024)S(1)} %pad_clamp_fusion), kind=kCustom, calls=%fused_computation | custom fusion | bytes 18883584 | tf_op jit(solution)/shard_map/gather | solution.py:144
  351.7 5.4 %fusion.17 = f32[2304,256]{1,0:T(8,128)S(1)} fusion(bf16[2304,2048]{1,0:T(8,128)(2,1)} %gather_fusion, bf16[256,2048]{1,0:T(8,128)(2,1)S(1)} %copy-done), kind=kOutput, calls=%fused_computation.47 | convolution fusion | flops 2415919104 | bytes 12845056 | tf_op jit(solution)/shard_map/dot_general | solution.py:77
  357.2 0.3 broadcast_in_dim.6
  357.5 0.0 copy-start.6
  357.5 8.9 %all_to_all.15 = f32[2,2304,256]{2,1,0:T(8,128)} all-to-all(f32[2,2304,256]{2,1,0:T(8,128)S(1)} %broadcast_in_dim.6), channel_id=1, replica_groups=mesh['seq_0'=8,'seq_1'=2,'img_0'=4,'img_1'=2,'fsdp'=2] {'fsdp'}, dimensions={0} | all-to-all | bytes 9437184 | tf_op jit(solution)/shard_map/all_to_all | solution.py:19
  366.4 0.8 broadcast_in_dim.7
  367.2 3.8 all-to-all-start.2
  371.1 4.5 reduce_sum.66
  375.6 0.0 all-to-all-done.2
  375.6 0.0 slice-start.2
  375.6 6.8 %fusion.5 = (bf16[2304,256]{1,0:T(8,128)(2,1)}, f32[2304,256]{1,0:T(8,128)S(1)}) fusion(f32[2304,256]{1,0:T(8,128)} %reduce_sum.66, f32[256]{0:T(256)S(1)} %copy-done.11, bf16[2304,1024]{1,0:T(8,128)(2,1)} %bitcast.36, bf16[1024,256]{1,0:T(8,128)(2,1)S(1)} %bitcast.38), kind=kOutput, calls=%fused_computation.16 | convolution fusion | flops 1214447616 | bytes 11142144 | tf_op jit(solution)/shard_map/dot_general | solution.py:139
  382.4 4.0 fusion.6
  386.4 2.0 reshape_reshape.7
  388.4 3.6 fusion.18
  392.0 2.0 reshape_reshape.6
  393.9 2.7 pad_maximum_fusion
  396.6 3.6 reshape.221
  400.3 0.0 reduce-scatter.2.cloned.1.call-update
  400.3 9.0 %scatter_custom_fusion = f32[4096]{0:T(1024)S(1)} fusion(s32[2304]{0:T(1024)S(1)} %fusion.13, f32[2304]{0:T(1024)S(1)} %broadcast.124, f32[]{:T(128)} %constant.22.clone.1), kind=kCustom, calls=%fused_computation.37 | custom fusion | bytes 16388 | tf_op jit(solution)/shard_map/scatter | solution.py:116
  409.3 0.1 dynamic_slice.28
  409.4 0.2 fusion.7
  409.7 0.2 dynamic_update_slice.13
  409.9 6.3 %copy.20 = f32[2304,512]{1,0:T(8,128)} copy(f32[2304,512]{0,1:T(8,128)} %bitcast.35) | data formatting | bytes 9437184 | tf_op jit(solution)/shard_map/reshape | solution.py:87
  416.3 3.2 fusion.16
  419.5 0.1 reshape.229
  419.6 0.1 reshape.230
  419.7 0.1 reshape.227
  419.8 0.1 reshape.228
  419.9 0.2 convert_reduce_fusion.1
  420.1 0.3 dynamic_update_slice.12
  420.3 23.4 %all-reduce = (f32[4096]{0:T(1024)S(1)}, f32[4096]{0:T(1024)S(1)}, f32[1024]{0:T(1024)S(1)}, f32[1024]{0:T(1024)S(1)}) all-reduce(f32[4096]{0:T(1024)S(1)} %dynamic_update_slice.12, f32[4096]{0:T(1024)S(1)} %dynamic_update_slice.13, ...), channel_id=1, replica_groups=mesh['seq_0'=8,'seq_1'=2,'img_0'=4,'img_1'=2,'fsdp'=2] {'seq_0'}, use_global_device_ids=true, to_apply=%region_7.8 | all-reduce | flops 10240 | bytes 81920 | tf_op jit(solution)/shard_map/psum | solution.py:66
  443.8 6.2 %all-reduce.4 = (f32[4096]{0:T(1024)S(1)}, f32[4096]{0:T(1024)S(1)}, f32[1024]{0:T(1024)S(1)}, f32[1024]{0:T(1024)S(1)}) all-reduce(f32[4096]{0:T(1024)S(1)} %get-tuple-element.8, f32[4096]{0:T(1024)S(1)} %get-tuple-element.9, ...), channel_id=1, replica_groups=mesh['seq_0'=8,'seq_1'=2,'img_0'=4,'img_1'=2,'fsdp'=2] {'seq_1'}, use_global_device_ids=true, to_apply=%region_8.9 | all-reduce | flops 10240 | bytes 81920 | tf_op jit(solution)/shard_map/psum | solution.py:66
  449.9 14.1 %all-reduce.1 = (f32[4096]{0:T(1024)S(1)}, f32[4096]{0:T(1024)S(1)}, f32[1024]{0:T(1024)S(1)}, f32[1024]{0:T(1024)S(1)}) all-reduce(f32[4096]{0:T(1024)S(1)} %get-tuple-element.24, f32[4096]{0:T(1024)S(1)} %get-tuple-element.25, ...), channel_id=1, replica_groups=mesh['seq_0'=8,'seq_1'=2,'img_0'=4,'img_1'=2,'fsdp'=2] {'img_0'}, use_global_device_ids=true, to_apply=%region_9.10 | all-reduce | flops 10240 | bytes 81920 | tf_op jit(solution)/shard_map/psum | solution.py:66
  464.0 10.6 %all-reduce.3 = (f32[4096]{0:T(1024)S(1)}, f32[4096]{0:T(1024)S(1)}, f32[1024]{0:T(1024)S(1)}, f32[1024]{0:T(1024)S(1)}) all-reduce(f32[4096]{0:T(1024)S(1)} %get-tuple-element.12, f32[4096]{0:T(1024)S(1)} %get-tuple-element.13, ...), channel_id=1, replica_groups=mesh['seq_0'=8,'seq_1'=2,'img_0'=4,'img_1'=2,'fsdp'=2] {'img_1'}, use_global_device_ids=true, to_apply=%region_10.11 | all-reduce | flops 10240 | bytes 81920 | tf_op jit(solution)/shard_map/psum | solution.py:66
  474.6 15.7 %all-reduce.2 = (f32[4096]{0:T(1024)}, f32[4096]{0:T(1024)}, f32[1024]{0:T(1024)}, f32[1024]{0:T(1024)}) all-reduce(f32[4096]{0:T(1024)S(1)} %get-tuple-element.20, f32[4096]{0:T(1024)S(1)} %get-tuple-element.21, f32[1024]{0:T(1024)S(1)} %get-tuple-element.22, ...), channel_id=1, replica_groups=mesh['seq_0'=8,'seq_1'=2,'img_0'=4,'img_1'=2,'fsdp'=2] {'fsdp'}, use_global_device_ids=true, to_apply=%region_11.12 | all-reduce | flops 10240 | bytes 81920 | tf_op jit(solution)/shard_map/psum | solution.py:66
  490.3 1.0 slice.13
  491.3 0.7 reshape.223
  492.0 0.8 slice.12
  492.9 0.6 reshape.222
  (46 shorter events, 0.3 us)
Async XLA Ops:
  7.2 344.6 %copy-start = (bf16[256,2048]{1,0:T(8,128)(2,1)S(1)}, bf16[256,2048]{1,0:T(8,128)(2,1)}, u32[]{:S(2)}) copy-start(bf16[256,2048]{1,0:T(8,128)(2,1)} %param.14) | copy-start | bytes 3145732
  7.2 44.5 %copy-start.7 = (bf16[1,72,1024]{2,1,0:T(8,128)(2,1)S(1)}, bf16[1,72,1024]{2,1,0:T(8,128)(2,1)}, u32[]{:S(2)}) copy-start(bf16[1,72,1024]{2,1,0:T(8,128)(2,1)} %param.9) | copy-start | bytes 442372
  7.2 44.4 %all-gather.5.cloned.1.call-start = ((), (), s32[]{:S(2)}) async-start(), calls=%async_computation.5 | async-start | bytes 3145728 | tf_op jit(solution)/shard_map/all_gather | solution.py:36
  7.9 317.5 %all-gather.7.cloned.1.call-start = ((), (), s32[]{:S(2)}) async-start(), calls=%async_computation.6 | async-start | bytes 18874368 | tf_op jit(solution)/shard_map/all_gather | solution.py:36
  54.4 8.2 %copy-start.12 = (s32[1,2]{1,0:T(1,128)S(1)}, s32[1,2]{1,0:T(1,128)}, u32[]{:S(2)}) copy-start(s32[1,2]{1,0:T(1,128)} %param.16) | copy-start | bytes 28
  54.4 8.4 %copy-start.9 = (f32[1024]{0:T(1024)S(1)}, f32[1024]{0:T(1024)}, u32[]{:S(2)}) copy-start(f32[1024]{0:T(1024)} %param.10) | copy-start | bytes 12292
  54.4 8.5 %copy-start.8 = (f32[1024]{0:T(1024)S(1)}, f32[1024]{0:T(1024)}, u32[]{:S(2)}) copy-start(f32[1024]{0:T(1024)} %param.11) | copy-start | bytes 12292
  54.4 8.7 %copy-start.10 = (s32[1,2304]{1,0:T(1,128)S(1)}, s32[1,2304]{1,0:T(1,128)}, u32[]{:S(2)}) copy-start(s32[1,2304]{1,0:T(1,128)} %param.17) | copy-start | bytes 27652
  54.4 165.6 %all-to-all-start = ((bf16[32,72,1024]{2,1,0:T(8,128)(2,1)}), bf16[32,72,1024]{2,1,0:T(8,128)(2,1)}, u32[]{:S(2)}, u32[]{:S(2)}) async-start(bf16[32,72,1024]{2,1,0:T(8,128)(2,1)} %stack.3), calls=%async_computation | async-start | bytes 9437184 | tf_op jit(solution)/shard_map/all_to_all | solution.py:131
  270.1 6.9 %copy-start.1 = (f32[2304,8,2,64]{0,3,2,1:T(8,128)S(1)}, f32[2304,8,2,64]{0,3,2,1:T(8,128)}, u32[]{:S(2)}) copy-start(f32[2304,8,2,64]{0,3,2,1:T(8,128)} %copy.21) | copy-start | bytes 28311556
  357.5 8.9 %copy-start.6 = (bf16[512,256]{1,0:T(8,128)(2,1)S(1)}, bf16[512,256]{1,0:T(8,128)(2,1)}, u32[]{:S(2)}) copy-start(bf16[512,256]{1,0:T(8,128)(2,1)} %param.12) | copy-start | bytes 786436
  367.2 8.4 %all-to-all-start.2 = ((bf16[2,512,256]{2,1,0:T(8,128)(2,1)}), bf16[2,512,256]{2,1,0:T(8,128)(2,1)S(1)}, u32[]{:S(2)}, u32[]{:S(2)}) async-start(bf16[2,512,256]{2,1,0:T(8,128)(2,1)} %broadcast_in_dim.7), calls=%async_computation.2 | async-start | bytes 1048576 | tf_op jit(solution)/shard_map/all_to_all | solution.py:19
  371.1 4.5 copy-start.11
  371.1 119.2 %reduce-scatter.2.cloned.1.call-start = ((), (), s32[]{:S(2)}) async-start(), calls=%async_computation.4 | async-start | bytes 2949120 | tf_op jit(solution)/shard_map/reduce_scatter | solution.py:56
  371.1 11.3 %slice-start = ((s8[9437184]{0:T(1024)(128)(4,1)}), s8[1048576]{0:T(1024)(128)(4,1)S(1)}, s32[]{:S(2)}) async-start(s8[9437184]{0:T(1024)(128)(4,1)} %bitcast.33), calls=%async_computation.7 | async-start | bytes 2097152
  375.6 6.8 %copy-start.4 = (bf16[2,512,256]{2,1,0:T(8,128)(2,1)}, bf16[2,512,256]{2,1,0:T(8,128)(2,1)S(1)}, u32[]{:S(2)}) copy-start(bf16[2,512,256]{2,1,0:T(8,128)(2,1)S(1)} %all-to-all-done.2) | copy-start | bytes 1572868
  375.6 6.8 %slice-start.1 = ((s8[9437184]{0:T(1024)(128)(4,1)}), s8[4194304]{0:T(1024)(128)(4,1)S(1)}, s32[]{:S(2)}) async-start(s8[9437184]{0:T(1024)(128)(4,1)} %bitcast.33), calls=%async_computation.8 | async-start | bytes 8388608
  375.6 6.8 %slice-start.2 = ((s8[9437184]{0:T(1024)(128)(4,1)}), s8[4194304]{0:T(1024)(128)(4,1)S(1)}, s32[]{:S(2)}) async-start(s8[9437184]{0:T(1024)(128)(4,1)} %bitcast.33), calls=%async_computation.9 | async-start | bytes 8388608
  400.3 9.1 %copy-start.2 = (bf16[1,256,2048]{2,1,0:T(8,128)(2,1)S(1)}, bf16[1,256,2048]{2,1,0:T(8,128)(2,1)}, u32[]{:S(2)}) copy-start(bf16[1,256,2048]{2,1,0:T(8,128)(2,1)} %param.15) | copy-start | bytes 3145732
  400.3 9.6 %copy-start.5 = (bf16[2,512,256]{2,1,0:T(8,128)(2,1)S(1)}, bf16[2,512,256]{2,1,0:T(8,128)(2,1)}, u32[]{:S(2)}) copy-start(bf16[2,512,256]{2,1,0:T(8,128)(2,1)} %copy-done.4) | copy-start | bytes 1572868
  409.9 6.3 %copy-start.3 = (bf16[2304,256]{1,0:T(8,128)(2,1)S(1)}, bf16[2304,256]{1,0:T(8,128)(2,1)}, u32[]{:S(2)}) copy-start(bf16[2304,256]{1,0:T(8,128)(2,1)} %get-tuple-element.30) | copy-start | bytes 3538948
Sparse Core Ops, SparseCore 0:
  9.8 41.7 all-gather.4
  53.4 271.9 all-gather.6
  400.4 80.3 reduce-scatter.1
